TPU v7x, 256 devices: a whole 4x4x8 slice. The times are simulated.
256 devices in a mesh: dp: 8 (over z_lo, core), vocab: 32 (over z_hi, x, y).
Axes of the slice: x: 4, y: 4, z: 8 (z_hi: 2, z_lo: 4; z = z_hi * 4 + z_lo), core: 2. Of those that a mesh axis runs over, the one named last changes fastest.
Arguments:
- policy_hidden: bfloat16 [1024, 4096], P('dp'), may hold values from -84 to 84
- policy_weight: bfloat16 [4096, 65536], P('dp', 'vocab'), may hold values from -0.09375 to 0.09375
- reference_hidden: bfloat16 [1024, 4096], P(('dp', 'vocab')), may hold values from -84 to 84
- reference_weight: bfloat16 [4096, 65536], P(None, ('dp', 'vocab')), may hold values from -0.09375 to 0.09375
- targets: int32 [1024], replicated, may hold values from 0 to 65535
- response_mask: int32 [1024], replicated, may hold values 0 or 1
- pair_index: int32 [32], replicated, may hold values from 0 to 31, each once
Outputs:
- hidden_grad: bfloat16 [1024, 4096], P('vocab', 'dp')
- weight_grad: bfloat16 [4096, 65536], P('dp', 'vocab')
- total_loss: float32 [], replicated
Inputs may be any that keep to these rules, and one draw needn't show every extreme that they name: `pair_index`: each number of 0 to 31 once; entries 2p and 2p + 1 are the chosen and the rejected sequence of pair p.
All inputs are finite; a program needn't handle non-finite values.
Results may differ from a plain program's by a relative error of at most 0.005.
The roundings to bfloat16 on the way count: a program that leaves them out, or rounds other values in their place, can miss the bound.
Values may be sent and summed in bfloat16 or wider, within the bound.
A program may use at most 128 MiB of HBM per device.

v0:
```python
import jax
import jax.numpy as jnp
from jax import lax
from jax.sharding import Mesh
from jax.sharding import PartitionSpec as P

SEQ_LEN = 32
DP = ("dp_0", "dp_1")
VOCAB = ("vocab_0", "vocab_1", "vocab_2")
DP_VOCAB = ("dp_0", "dp_1", "vocab_0", "vocab_1", "vocab_2")
beta = 0.1
loss_scale = 4096.0


def all_in_one(value, axis):
    leaves = jax.tree.leaves(value)
    order = sorted(range(len(leaves)), key=lambda k: -leaves[k].size)
    width = (1, *leaves[order[0]].shape)[-1]
    lines = [
        jnp.pad(leaves[k].reshape(-1), (0, -leaves[k].size % width)).reshape(-1, width)
        for k in order
    ]
    both, at, found = (lax.all_gather(jnp.concatenate(lines), axis), 0, {})
    for k, line in zip(order, lines):
        slab = both[:, at : at + len(line)].reshape(len(both), -1)
        found[k] = slab[:, : leaves[k].size].reshape(-1, *leaves[k].shape)
        at += len(line)
    numbers = iter(range(len(leaves)))
    return jax.tree.map(lambda _: found[next(numbers)], value)


def merged_by_axis(value, axes, combine):
    for axis in axes:
        pieces = all_in_one(value, axis)
        value = jax.tree.map(lambda part: part[0], pieces)
        for k in range(1, lax.axis_size(axis)):
            value = combine(value, jax.tree.map(lambda part: part[k], pieces))
    return value


def in_blocks(value, dim, peers):
    shape = value.shape
    tiles = value.reshape(*shape[:dim], peers, shape[dim] // peers, *shape[dim + 1 :])
    return jnp.moveaxis(tiles, dim, 0)


def sum_at_owner(value, axis, dim):
    peers = lax.axis_size(axis)
    tiles = lax.all_to_all(in_blocks(value, dim, peers), axis, 0, 0, tiled=True)
    return jnp.sum(tiles, axis=0)


def pair_terms(log_ratio, pair_index):
    chosen = pair_index[0::2]
    rejected = pair_index[1::2]
    margin = beta * (log_ratio[chosen] - log_ratio[rejected])
    pair_count = chosen.shape[0]
    total_loss = jnp.sum(jax.nn.softplus(-margin)) / pair_count
    weight = -beta * loss_scale * jax.nn.sigmoid(-margin) / pair_count
    numbers = jnp.arange(log_ratio.shape[0], dtype=jnp.int32)[:, None]
    factor = jnp.sum(
        jnp.where(numbers == chosen[None, :], weight[None, :], 0.0)
        - jnp.where(numbers == rejected[None, :], weight[None, :], 0.0),
        axis=1,
    )
    return (total_loss, factor)


def local_pick(logits, targets, offset, axis):
    column_ids = lax.broadcasted_iota(jnp.int32, logits.shape, axis)
    shifted = targets - offset
    wanted = shifted[:, None] if axis == 1 else shifted[None, :]
    return jnp.sum(jnp.where(column_ids == wanted, logits, 0.0), axis=axis)


def merge_pair(earlier, later):
    largest = jnp.maximum(earlier[0], later[0])
    exp_total = earlier[1] * jnp.exp(earlier[0] - largest) + later[1] * jnp.exp(later[0] - largest)
    return (largest, exp_total, earlier[2] + later[2])


def merge_heads(earlier, later):
    return merge_pair(earlier[0:3], later[0:3]) + merge_pair(earlier[3:6], later[3:6])


def local(
    policy_hidden,
    policy_weight,
    reference_hidden,
    reference_weight,
    targets,
    response_mask,
    pair_index,
):
    data_index = lax.axis_index(DP)
    vocab_index = lax.axis_index(VOCAB)
    vocab_devices = lax.axis_size(VOCAB)
    data_devices = lax.axis_size(DP)
    policy_width = policy_weight.shape[1]
    reference_width = reference_weight.shape[1]
    active = response_mask.astype(jnp.float32)
    columns = lax.all_to_all(policy_hidden, DP, split_axis=1, concat_axis=0, tiled=True)
    reference_rows = reference_hidden
    for axis in ("dp_0", "vocab_0", "vocab_2", "vocab_1", "dp_1"):
        reference_rows = lax.all_gather(reference_rows, axis, axis=0, tiled=True)
    reference_logits = jnp.dot(reference_rows, reference_weight, preferred_element_type=jnp.float32)
    reference_targets = targets.reshape(4, 2, 2, 4, 4, 4).transpose(1, 3, 4, 2, 0, 5).reshape(-1)

    def in_order(value):
        return value.reshape(2, 4, 4, 2, 4, 4).transpose(4, 0, 3, 1, 2, 5).reshape(-1)

    reference_offset = (data_index * vocab_devices + vocab_index) * reference_width
    reference_top = jnp.max(reference_logits, axis=1)
    reference_pick = local_pick(reference_logits, reference_targets, reference_offset, 1)
    slice_width = policy_width // data_devices
    weight_block = policy_weight
    policy_logits = lax.psum_scatter(
        lax.dot_general(
            weight_block, columns, (((0,), (1,)), ((), ())), preferred_element_type=jnp.float32
        ),
        DP,
        scatter_dimension=0,
        tiled=True,
    )
    policy_offset = vocab_index * policy_width + data_index * slice_width
    policy_top = jnp.max(policy_logits, axis=0)
    policy_pick = local_pick(policy_logits, targets, policy_offset, 0)
    local_stats = (
        policy_top,
        jnp.sum(jnp.exp(policy_logits - policy_top[None, :]), axis=0),
        policy_pick,
        in_order(reference_top),
        in_order(jnp.sum(jnp.exp(reference_logits - reference_top[:, None]), axis=1)),
        in_order(reference_pick),
    )
    merged = merged_by_axis(local_stats, DP_VOCAB, merge_heads)
    policy_total = merged[0] + jnp.log(merged[1])
    reference_logp = merged[5] - merged[3] - jnp.log(merged[4])
    log_ratio = jnp.sum(
        (active * (merged[2] - policy_total - reference_logp)).reshape(-1, SEQ_LEN), axis=1
    )
    total_loss, factor = pair_terms(log_ratio, pair_index)
    token_scale = active * jnp.repeat(factor, SEQ_LEN)
    row_ids = lax.broadcasted_iota(jnp.int32, policy_logits.shape, 0)
    onehot = (row_ids == (targets - policy_offset)[None, :]).astype(jnp.float32)
    logit_grad = (
        token_scale[None, :] * (onehot - jnp.exp(policy_logits - policy_total[None, :]))
    ).astype(jnp.bfloat16)
    segment = lax.all_gather(logit_grad, DP, axis=0, tiled=True)
    weight_block = policy_weight
    column_grad = lax.dot_general(
        columns, segment, (((0,), (1,)), ((), ())), preferred_element_type=jnp.float32
    )
    hidden_part = lax.dot_general(
        segment, weight_block, (((0,), (1,)), ((), ())), preferred_element_type=jnp.float32
    )
    weight_grad, hidden_part = (column_grad, hidden_part)
    hidden_grad = sum_at_owner(hidden_part, VOCAB, 0)
    return (hidden_grad.astype(jnp.bfloat16), weight_grad.astype(jnp.bfloat16), total_loss)


def solution(mesh):
    torus = Mesh(
        mesh.devices.reshape(4, 2, 2, 4, 4), ("dp_0", "dp_1", "vocab_0", "vocab_1", "vocab_2")
    )
    in_specs = (P(DP, None), P(DP, VOCAB), P(DP_VOCAB, None), P(None, DP_VOCAB), P(), P(), P())
    out_specs = (P(VOCAB, DP), P(DP, VOCAB), P())
    return jax.shard_map(local, mesh=torus, in_specs=in_specs, out_specs=out_specs, check_vma=False)
```

profile of v0, /device:TPU:38, one launch (start us, length us, event | category | flops | bytes accessed | tf_op | source)
XLA Modules:
  0.0 438.4 jit_solution(6761728711644219476)
XLA Ops:
  8.1 14.9 %all-gather.5 = bf16[4,4,4096]{2,1,0:T(4,128)(2,1)S(1)} all-gather(bf16[1,4,4096]{2,1,0:T(4,128)(2,1)} %bitcast.468), channel_id=1, replica_groups=mesh['dp_0'=4,'dp_1'=2,'vocab_0'=2,'vocab_1'=4,'vocab_2'=4] {'dp_0'}, dimensions={0}, use_global_device_ids=true | all-gather | bytes 163840 | tf_op jit(solution)/shard_map/all_gather | solution.py:105
  23.0 9.7 %all_gather.49 = bf16[32,4096]{1,0:T(8,128)(2,1)} all-gather(bf16[16,4096]{1,0:T(8,128)(2,1)S(1)} %reshape.1628), channel_id=1, replica_groups=mesh['dp_0'=4,'dp_1'=2,'vocab_0'=2,'vocab_1'=4,'vocab_2'=4] {'vocab_0'}, dimensions={0}, use_global_device_ids=true | all-gather | bytes 393216 | tf_op jit(solution)/shard_map/all_gather | solution.py:105
  32.8 28.1 %all-gather.16.cloned.1.call-done = bf16[128,4096]{1,0:T(8,128)(2,1)} async-done(((bf16[32,4096]{1,0:T(8,128)(2,1)}), bf16[128,4096]{1,0:T(8,128)(2,1)}) %all-gather.16.cloned.1.call-update) | async-done | bytes 1048592 | tf_op jit(solution)/shard_map/all_gather | solution.py:105
  61.0 51.3 %all-gather.18.cloned.1.call-done = bf16[512,4096]{1,0:T(8,128)(2,1)} async-done(((bf16[128,4096]{1,0:T(8,128)(2,1)}), bf16[512,4096]{1,0:T(8,128)(2,1)}) %all-gather.18.cloned.1.call-update) | async-done | bytes 4194320 | tf_op jit(solution)/shard_map/all_gather | solution.py:105
  113.5 1.3 copy.26
  114.8 29.5 %all_to_all.24 = bf16[128,8,512]{0,2,1:T(8,128)(2,1)S(1)} all-to-all(bf16[128,8,512]{0,2,1:T(8,128)(2,1)} %bitcast.454), channel_id=1, replica_groups=mesh['dp_0'=4,'dp_1'=2,'vocab_0'=2,'vocab_1'=4,'vocab_2'=4] {'dp_0','dp_1'}, dimensions={1} | all-to-all | bytes 2097152 | tf_op jit(solution)/shard_map/all_to_all | solution.py:102
  144.3 1.3 copy.27
  145.6 6.8 %fusion.94 = f32[2048,1024]{1,0:T(8,128)} fusion(bf16[512,2048]{1,0:T(8,128)(2,1)S(1)} %copy-done, bf16[1024,512]{1,0:T(8,128)(2,1)} %bitcast.456), kind=kOutput, calls=%fused_computation.187 | convolution fusion | flops 2147483648 | bytes 11534336 | tf_op jit(solution)/shard_map/dot_general | solution.py:118
  153.9 6.4 %fusion.93 = (f32[1024]{0:T(1024)S(1)}, f32[1024,256]{0,1:T(8,128)S(1)}) fusion(bf16[1024,4096]{1,0:T(8,128)(2,1)} %all-gather.20.cloned.1.call-done, bf16[4096,256]{1,0:T(8,128)(2,1)} %param.10), kind=kOutput, calls=%fused_computation.186 | convolution fusion | flops 2147744768 | bytes 11538432 | tf_op jit(solution)/shard_map/dot_general | solution.py:106
  161.8 84.9 %reduce-scatter.2.cloned.1.call-done = f32[256,1024]{1,0:T(8,128)} async-done(((f32[2048,1024]{1,0:T(8,128)}), f32[256,1024]{1,0:T(8,128)}) %reduce-scatter.2.cloned.1.call-update) | async-done | bytes 1048592 | tf_op jit(solution)/shard_map/reduce_scatter | solution.py:117
  246.6 1.3 reduce_max.18
  248.0 1.6 select_reduce_fusion.1
  249.6 14.0 %all-gather.6 = f32[4,6,1024]{2,1,0:T(8,128)S(1)} all-gather(f32[1,6,1024]{2,1,0:T(8,128)S(1)} %bitcast.462), channel_id=2, replica_groups=mesh['dp_0'=4,'dp_1'=2,'vocab_0'=2,'vocab_1'=4,'vocab_2'=4] {'dp_0'}, dimensions={0}, use_global_device_ids=true | all-gather | bytes 122880 | tf_op jit(solution)/shard_map/all_gather | solution.py:23
  263.8 1.9 all-gather.7
  265.8 8.5 %all-gather.8 = f32[2,6,1024]{2,1,0:T(8,128)S(1)} all-gather(f32[1,6,1024]{2,1,0:T(8,128)S(1)} %bitcast.464), channel_id=4, replica_groups=mesh['dp_0'=4,'dp_1'=2,'vocab_0'=2,'vocab_1'=4,'vocab_2'=4] {'vocab_0'}, dimensions={0}, use_global_device_ids=true | all-gather | bytes 73728 | tf_op jit(solution)/shard_map/all_gather | solution.py:23
  274.4 12.0 %all-gather.9 = f32[4,6,1024]{2,1,0:T(8,128)S(1)} all-gather(f32[1,6,1024]{2,1,0:T(8,128)S(1)} %bitcast.465), channel_id=5, replica_groups=mesh['dp_0'=4,'dp_1'=2,'vocab_0'=2,'vocab_1'=4,'vocab_2'=4] {'vocab_1'}, dimensions={0}, use_global_device_ids=true | all-gather | bytes 122880 | tf_op jit(solution)/shard_map/all_gather | solution.py:23
  286.6 12.6 %all-gather.10 = f32[4,6,1024]{2,1,0:T(8,128)S(1)} all-gather(f32[1,6,1024]{2,1,0:T(8,128)S(1)} %bitcast.466), channel_id=6, replica_groups=mesh['dp_0'=4,'dp_1'=2,'vocab_0'=2,'vocab_1'=4,'vocab_2'=4] {'vocab_2'}, dimensions={0}, use_global_device_ids=true | all-gather | bytes 122880 | tf_op jit(solution)/shard_map/all_gather | solution.py:23
  302.8 51.4 %all-gather.22.cloned.1.call-done = bf16[2048,1024]{1,0:T(8,128)(2,1)} async-done(((bf16[256,1024]{1,0:T(8,128)(2,1)}), bf16[2048,1024]{1,0:T(8,128)(2,1)}) %all-gather.22.cloned.1.call-update) | async-done | bytes 4194320 | tf_op jit(solution)/shard_map/all_gather | solution.py:149
  354.2 5.9 %fusion.95 = f32[1024,512]{1,0:T(8,128)} fusion(bf16[2048,1024]{1,0:T(8,128)(2,1)} %all-gather.22.cloned.1.call-done, bf16[512,2048]{1,0:T(8,128)(2,1)S(1)} %copy-done), kind=kOutput, calls=%fused_computation.188 | convolution fusion | flops 2147483648 | bytes 8388608 | tf_op jit(solution)/shard_map/dot_general | solution.py:154
  360.1 13.1 %all-to-all-start.1 = ((f32[32,32,512]{2,1,0:T(8,128)}), f32[32,32,512]{2,1,0:T(8,128)}, u32[]{:S(2)}, u32[]{:S(2)}) async-start(f32[32,32,512]{2,1,0:T(8,128)} %bitcast.455), calls=%async_computation.2 | async-start | bytes 4194304 | tf_op jit(solution)/shard_map/all_to_all | solution.py:49
  373.9 5.9 %fusion = bf16[512,2048]{0,1:T(8,128)(2,1)} fusion(bf16[2048,1024]{1,0:T(8,128)(2,1)} %all-gather.22.cloned.1.call-done, bf16[1024,512]{1,0:T(8,128)(2,1)S(1)} %bitcast.457), kind=kOutput, calls=%fused_computation.3 | convolution fusion | flops 2148532224 | bytes 7340032 | tf_op jit(solution)/shard_map/dot_general | solution.py:151
  379.8 3.9 copy.32
  383.7 44.1 %all-to-all-done.1 = f32[32,32,512]{2,1,0:T(8,128)} async-done(((f32[32,32,512]{2,1,0:T(8,128)}), f32[32,32,512]{2,1,0:T(8,128)}, u32[]{:S(2)}, u32[]{:S(2)}) %all-to-all-start.1) | async-done | bytes 2097184 | tf_op jit(solution)/shard_map/all_to_all | solution.py:49
  427.8 2.4 reduce_sum.78
  (72 shorter events, 8.4 us)
Async XLA Ops:
  8.0 137.6 %copy-start = (bf16[512,2048]{1,0:T(8,128)(2,1)S(1)}, bf16[512,2048]{1,0:T(8,128)(2,1)}, u32[]{:S(2)}) copy-start(bf16[512,2048]{1,0:T(8,128)(2,1)} %param.8) | copy-start | bytes 6291460
  8.0 52.9 %all-gather.16.cloned.1.call-start = ((), (), s32[]{:S(2)}) async-start(), calls=%async_computation.4 | async-start | bytes 1310720 | tf_op jit(solution)/shard_map/all_gather | solution.py:105
  32.8 79.5 %all-gather.18.cloned.1.call-start = ((), (), s32[]{:S(2)}) async-start(), calls=%async_computation.5 | async-start | bytes 5242880 | tf_op jit(solution)/shard_map/all_gather | solution.py:105
  60.9 93.0 %all-gather.20.cloned.1.call-start = ((), (), s32[]{:S(2)}) async-start(), calls=%async_computation.6 | async-start | bytes 12582912 | tf_op jit(solution)/shard_map/all_gather | solution.py:105
  112.3 1.2 copy-start.2
  112.3 134.4 %reduce-scatter.2.cloned.1.call-start = ((), (), s32[]{:S(2)}) async-start(), calls=%async_computation.3 | async-start | bytes 9437184 | tf_op jit(solution)/shard_map/reduce_scatter | solution.py:117
  152.5 0.7 copy-start.6
  152.5 0.9 copy-start.5
  152.5 201.7 %all-gather.22.cloned.1.call-start = ((), (), s32[]{:S(2)}) async-start(), calls=%async_computation.7 | async-start | bytes 4718592 | tf_op jit(solution)/shard_map/all_gather | solution.py:149
  161.5 137.7 %copy-start.4 = (s32[1024]{0:T(1024)S(1)}, s32[1024]{0:T(1024)}, u32[]{:S(2)}) copy-start(s32[1024]{0:T(1024)} %param.12) | copy-start | bytes 12292
  247.9 53.8 %copy-start.1 = (f32[256,1024]{1,0:T(8,128)S(1)}, f32[256,1024]{1,0:T(8,128)}, u32[]{:S(2)}) copy-start(f32[256,1024]{1,0:T(8,128)} %reduce-scatter.2.cloned.1.call-done) | copy-start | bytes 3145732
  360.1 13.8 %copy-start.3 = (bf16[8,128,512]{2,1,0:T(8,128)(2,1)S(1)}, bf16[8,128,512]{2,1,0:T(8,128)(2,1)}, u32[]{:S(2)}) copy-start(bf16[8,128,512]{2,1,0:T(8,128)(2,1)} %copy.27) | copy-start | bytes 3145732
  360.1 67.7 %all-to-all-start.1 = ((f32[32,32,512]{2,1,0:T(8,128)}), f32[32,32,512]{2,1,0:T(8,128)}, u32[]{:S(2)}, u32[]{:S(2)}) async-start(f32[32,32,512]{2,1,0:T(8,128)} %bitcast.455), calls=%async_computation.2 | async-start | bytes 4194304 | tf_op jit(solution)/shard_map/all_to_all | solution.py:49
Sparse Core Ops, SparseCore 0:
  32.9 27.9 all-gather.15
  62.7 49.5 all-gather.17
  114.1 27.0 all-gather.19
Sparse Core Ops, SparseCore 1:
  152.6 94.0 reduce-scatter.1
  302.9 51.2 all-gather.21
where the time goes:
time: 439 us; the launch traced here: 438 us
  waiting for transfers between devices  260 us (59%)
  blocking collectives  103 us (23%)
  matrix products  25 us (6%)
  between operations  17.2 us (4%)
  starting transfers between devices  13.3 us (3%)
  local copies, waits for them, and re-layouts  11.9 us (3%)
  other arithmetic  7.93 us (2%)
    reduce_scatter x1, waiting for transfers between devices, local(): lax.psum_scatter(lax.dot_general(weight_block, columns, (((0,), (1,)), ((...  84.9 us
    all_gather x3, waiting for transfers between devices, local(): reference_rows = lax.all_gather(reference_rows, axis, axis=0, tiled=True)  79.4 us
    all_gather x1, waiting for transfers between devices, local(): segment = lax.all_gather(logit_grad, DP, axis=0, tiled=True)  51.4 us
    all_gather x5, blocking collectives, all_in_one(): both, at, found = (lax.all_gather(jnp.concatenate(lines), axis), 0, {})  49 us
    all_to_all x1, waiting for transfers between devices, sum_at_owner(): tiles = lax.all_to_all(in_blocks(value, dim, peers), axis, 0, 0, tiled=True)  44.1 us
    all_to_all x1, blocking collectives, local(): lax.all_to_all(policy_hidden, DP, split_axis=1, concat_axis=0, tiled=True)  29.5 us
    all_gather x2, blocking collectives, local(): reference_rows = lax.all_gather(reference_rows, axis, axis=0, tiled=True)  24.6 us
    all_to_all x1, starting transfers between devices, sum_at_owner(): tiles = lax.all_to_all(in_blocks(value, dim, peers), axis, 0, 0, tiled=True)  13.1 us
  transfers between devices with their start and end apart: 6, of which 5 were waited for; matrix products, arithmetic and copies ran while one was open for 6% of the time, Pallas kernels for 0%

commit v1 on v0

--- a/solution.py
+++ b/solution.py
@@ -102,7 +102,13 @@
     columns = lax.all_to_all(policy_hidden, DP, split_axis=1, concat_axis=0, tiled=True)
     reference_rows = reference_hidden
     for axis in ("dp_0", "vocab_0", "vocab_2", "vocab_1", "dp_1"):
-        reference_rows = lax.all_gather(reference_rows, axis, axis=0, tiled=True)
+
+        def manage_records(inputs, dev_axis):
+            r_now = jnp.stack([inputs for _ in range(lax.axis_size(dev_axis))])
+            v1 = lax.all_to_all(r_now, dev_axis, 0, 0)
+            return jnp.concatenate(v1, axis=0)
+
+        reference_rows = manage_records(reference_rows, axis)
     reference_logits = jnp.dot(reference_rows, reference_weight, preferred_element_type=jnp.float32)
     reference_targets = targets.reshape(4, 2, 2, 4, 4, 4).transpose(1, 3, 4, 2, 0, 5).reshape(-1)
 

time: 439 us -> 360 us (0.82)
  waiting for transfers between devices: 260 us -> 136 us
  blocking collectives: 103 us -> 137 us
  other arithmetic: 7.93 us -> 15.4 us
  starting transfers between devices: 13.3 us -> 18.7 us
    reduce_scatter x1, waiting for transfers between devices: 84.9 us -> 0.01 us  [local(): lax.psum_scatter(lax.dot_general(weight_block, columns, (((0,), (1,)), ((...]
    all_gather x3 -> x0, waiting for transfers between devices: 79.4 us -> none  [local(): reference_rows = lax.all_gather(reference_rows, axis, axis=0, tiled=True)]
    all_to_all x0 -> x4, blocking collectives: none -> 60.1 us  [manage_records(): v1 = lax.all_to_all(r_now, dev_axis, 0, 0)]
    all_to_all x0 -> x1, waiting for transfers between devices: none -> 43.1 us  [manage_records(): v1 = lax.all_to_all(r_now, dev_axis, 0, 0)]
    all_gather x2 -> x0, blocking collectives: 24.6 us -> none  [local(): reference_rows = lax.all_gather(reference_rows, axis, axis=0, tiled=True)]
    another operation x0 -> x2, other arithmetic: none -> 7.47 us  [manage_records(): r_now = jnp.stack([inputs for _ in range(lax.axis_size(dev_axis))])]
    all_to_all x0 -> x1, starting transfers between devices: none -> 5.39 us  [manage_records(): v1 = lax.all_to_all(r_now, dev_axis, 0, 0)]
  transfers between devices with their start and end apart: 6 -> 4, of which waited for: 5 -> 3; matrix products, arithmetic and copies ran while one was open for 6% -> 7% of each run, Pallas kernels for 0% -> 0%
where the time goes in v1:
time: 360 us; the launch traced here: 359 us
  blocking collectives  137 us (38%)
  waiting for transfers between devices  136 us (38%)
  matrix products  21.1 us (6%)
  starting transfers between devices  18.7 us (5%)
  between operations  16.1 us (4%)
  other arithmetic  15.4 us (4%)
  local copies, waits for them, and re-layouts  14.6 us (4%)
    all_to_all x4, blocking collectives, manage_records(): v1 = lax.all_to_all(r_now, dev_axis, 0, 0)  60.1 us
    all_gather x1, waiting for transfers between devices, local(): segment = lax.all_gather(logit_grad, DP, axis=0, tiled=True)  48.5 us
    all_gather x5, blocking collectives, all_in_one(): both, at, found = (lax.all_gather(jnp.concatenate(lines), axis), 0, {})  47 us
    all_to_all x1, waiting for transfers between devices, sum_at_owner(): tiles = lax.all_to_all(in_blocks(value, dim, peers), axis, 0, 0, tiled=True)  44.1 us
    all_to_all x1, waiting for transfers between devices, manage_records(): v1 = lax.all_to_all(r_now, dev_axis, 0, 0)  43.1 us
    all_to_all x1, blocking collectives, local(): lax.all_to_all(policy_hidden, DP, split_axis=1, concat_axis=0, tiled=True)  30.3 us
    all_to_all x1, starting transfers between devices, sum_at_owner(): tiles = lax.all_to_all(in_blocks(value, dim, peers), axis, 0, 0, tiled=True)  13.2 us
    another operation x2, other arithmetic, manage_records(): r_now = jnp.stack([inputs for _ in range(lax.axis_size(dev_axis))])  7.47 us
  transfers between devices with their start and end apart: 4, of which 3 were waited for; matrix products, arithmetic and copies ran while one was open for 7% of the time, Pallas kernels for 0%

profile of v1, /device:TPU:38, one launch (start us, length us, event | category | flops | bytes accessed | tf_op | source)
XLA Modules:
  0.0 359.0 jit_solution(1359510357651416290)
XLA Ops:
  7.2 2.4 copy.26
  9.6 30.3 %all_to_all.49 = bf16[128,8,512]{0,2,1:T(8,128)(2,1)S(1)} all-to-all(bf16[128,8,512]{0,2,1:T(8,128)(2,1)} %bitcast.459), channel_id=1, replica_groups=mesh['dp_0'=4,'dp_1'=2,'vocab_0'=2,'vocab_1'=4,'vocab_2'=4] {'dp_0','dp_1'}, dimensions={1} | all-to-all | bytes 2097152 | tf_op jit(solution)/shard_map/all_to_all | solution.py:102
  41.2 6.8 %fusion.94 = f32[2048,1024]{1,0:T(8,128)} fusion(bf16[512,2048]{1,0:T(8,128)(2,1)S(1)} %copy-done, bf16[1024,512]{1,0:T(8,128)(2,1)} %bitcast.462), kind=kOutput, calls=%fused_computation.189 | convolution fusion | flops 2147483648 | bytes 11534336 | tf_op jit(solution)/shard_map/dot_general | solution.py:124
  48.8 9.8 %all_to_all.50 = bf16[4,4,4096]{2,1,0:T(4,128)(2,1)S(1)} all-to-all(bf16[4,4,4096]{2,1,0:T(4,128)(2,1)S(1)} %stack.19), channel_id=1, replica_groups=mesh['dp_0'=4,'dp_1'=2,'vocab_0'=2,'vocab_1'=4,'vocab_2'=4] {'dp_0'}, dimensions={0} | all-to-all | bytes 262144 | tf_op jit(solution)/shard_map/all_to_all | solution.py:108
  58.8 20.9 %all_to_all.51 = bf16[2,16,4096]{2,1,0:T(8,128)(2,1)S(1)} all-to-all(bf16[2,16,4096]{2,1,0:T(8,128)(2,1)S(1)} %pad_maximum_fusion.1), channel_id=1, replica_groups=mesh['dp_0'=4,'dp_1'=2,'vocab_0'=2,'vocab_1'=4,'vocab_2'=4] {'vocab_0'}, dimensions={0} | all-to-all | bytes 524288 | tf_op jit(solution)/shard_map/all_to_all | solution.py:108
  79.8 17.2 %all_to_all.52 = bf16[4,32,4096]{2,1,0:T(8,128)(2,1)S(1)} all-to-all(bf16[4,32,4096]{2,1,0:T(8,128)(2,1)S(1)} %stack.21), channel_id=1, replica_groups=mesh['dp_0'=4,'dp_1'=2,'vocab_0'=2,'vocab_1'=4,'vocab_2'=4] {'vocab_2'}, dimensions={0} | all-to-all | bytes 2097152 | tf_op jit(solution)/shard_map/all_to_all | solution.py:108
  96.9 2.5 stack.22
  99.4 5.4 %all-to-all-start.4 = ((bf16[4,128,4096]{2,1,0:T(8,128)(2,1)}), bf16[4,128,4096]{2,1,0:T(8,128)(2,1)}, u32[]{:S(2)}, u32[]{:S(2)}) async-start(bf16[4,128,4096]{2,1,0:T(8,128)(2,1)} %stack.22), calls=%async_computation.5 | async-start | bytes 8388608 | tf_op jit(solution)/shard_map/all_to_all | solution.py:108
  105.5 43.1 %all-to-all-done.4 = bf16[4,128,4096]{2,1,0:T(8,128)(2,1)} async-done(((bf16[4,128,4096]{2,1,0:T(8,128)(2,1)}), bf16[4,128,4096]{2,1,0:T(8,128)(2,1)}, u32[]{:S(2)}, u32[]{:S(2)}) %all-to-all-start.4) | async-done | bytes 4194336 | tf_op jit(solution)/shard_map/all_to_all | solution.py:108
  148.6 7.4 %pad_maximum_fusion = bf16[2,512,4096]{2,1,0:T(8,128)(2,1)} fusion(bf16[1,512,4096]{2,1,0:T(8,128)(2,1)} %bitcast.8), kind=kLoop, calls=%fused_computation.2 | loop fusion | flops 4194304 | bytes 12582912 | tf_op jit(solution)/shard_map/stack | solution.py:107
  156.1 12.2 %all_to_all.53 = bf16[2,512,4096]{2,1,0:T(8,128)(2,1)S(1)} all-to-all(bf16[2,512,4096]{2,1,0:T(8,128)(2,1)} %pad_maximum_fusion), channel_id=1, replica_groups=mesh['dp_0'=4,'dp_1'=2,'vocab_0'=2,'vocab_1'=4,'vocab_2'=4] {'dp_1'}, dimensions={0} | all-to-all | bytes 16777216 | tf_op jit(solution)/shard_map/all_to_all | solution.py:108
  168.3 2.4 fusion.93
  175.1 12.4 %all-gather.5 = f32[4,6,1024]{2,1,0:T(8,128)S(1)} all-gather(f32[1,6,1024]{2,1,0:T(8,128)S(1)} %bitcast.468), channel_id=2, replica_groups=mesh['dp_0'=4,'dp_1'=2,'vocab_0'=2,'vocab_1'=4,'vocab_2'=4] {'dp_0'}, dimensions={0}, use_global_device_ids=true | all-gather | bytes 122880 | tf_op jit(solution)/shard_map/all_gather | solution.py:23
  187.7 1.9 all-gather.6
  189.7 8.5 %all-gather.7 = f32[2,6,1024]{2,1,0:T(8,128)S(1)} all-gather(f32[1,6,1024]{2,1,0:T(8,128)S(1)} %bitcast.470), channel_id=4, replica_groups=mesh['dp_0'=4,'dp_1'=2,'vocab_0'=2,'vocab_1'=4,'vocab_2'=4] {'vocab_0'}, dimensions={0}, use_global_device_ids=true | all-gather | bytes 73728 | tf_op jit(solution)/shard_map/all_gather | solution.py:23
  198.3 12.1 %all-gather.8 = f32[4,6,1024]{2,1,0:T(8,128)S(1)} all-gather(f32[1,6,1024]{2,1,0:T(8,128)S(1)} %bitcast.471), channel_id=5, replica_groups=mesh['dp_0'=4,'dp_1'=2,'vocab_0'=2,'vocab_1'=4,'vocab_2'=4] {'vocab_1'}, dimensions={0}, use_global_device_ids=true | all-gather | bytes 122880 | tf_op jit(solution)/shard_map/all_gather | solution.py:23
  210.6 12.2 %all-gather.9 = f32[4,6,1024]{2,1,0:T(8,128)S(1)} all-gather(f32[1,6,1024]{2,1,0:T(8,128)S(1)} %bitcast.472), channel_id=6, replica_groups=mesh['dp_0'=4,'dp_1'=2,'vocab_0'=2,'vocab_1'=4,'vocab_2'=4] {'vocab_2'}, dimensions={0}, use_global_device_ids=true | all-gather | bytes 122880 | tf_op jit(solution)/shard_map/all_gather | solution.py:23
  226.4 48.5 %all-gather.12.cloned.1.call-done = bf16[2048,1024]{1,0:T(8,128)(2,1)} async-done(((bf16[256,1024]{1,0:T(8,128)(2,1)}), bf16[2048,1024]{1,0:T(8,128)(2,1)}) %all-gather.12.cloned.1.call-update) | async-done | bytes 4194320 | tf_op jit(solution)/shard_map/all_gather | solution.py:155
  275.0 5.9 %fusion.95 = f32[1024,512]{1,0:T(8,128)} fusion(bf16[2048,1024]{1,0:T(8,128)(2,1)} %all-gather.12.cloned.1.call-done, bf16[512,2048]{1,0:T(8,128)(2,1)S(1)} %copy-done), kind=kOutput, calls=%fused_computation.190 | convolution fusion | flops 2147483648 | bytes 8388608 | tf_op jit(solution)/shard_map/dot_general | solution.py:160
  280.9 13.2 %all-to-all-start.6 = ((f32[32,32,512]{2,1,0:T(8,128)}), f32[32,32,512]{2,1,0:T(8,128)}, u32[]{:S(2)}, u32[]{:S(2)}) async-start(f32[32,32,512]{2,1,0:T(8,128)} %bitcast.460), calls=%async_computation.7 | async-start | bytes 4194304 | tf_op jit(solution)/shard_map/all_to_all | solution.py:49
  294.8 5.9 %fusion = bf16[512,2048]{0,1:T(8,128)(2,1)} fusion(bf16[2048,1024]{1,0:T(8,128)(2,1)} %all-gather.12.cloned.1.call-done, bf16[1024,512]{1,0:T(8,128)(2,1)S(1)} %bitcast.463), kind=kOutput, calls=%fused_computation.4 | convolution fusion | flops 2148532224 | bytes 7340032 | tf_op jit(solution)/shard_map/dot_general | solution.py:157
  300.7 3.9 %copy.32 = bf16[512,2048]{1,0:T(8,128)(2,1)} copy(bf16[512,2048]{0,1:T(8,128)(2,1)} %fusion) | data formatting | bytes 4194304
  304.6 44.1 %all-to-all-done.6 = f32[32,32,512]{2,1,0:T(8,128)} async-done(((f32[32,32,512]{2,1,0:T(8,128)}), f32[32,32,512]{2,1,0:T(8,128)}, u32[]{:S(2)}, u32[]{:S(2)}) %all-to-all-start.6) | async-done | bytes 2097184 | tf_op jit(solution)/shard_map/all_to_all | solution.py:49
  348.7 2.4 reduce_sum.78
  (74 shorter events, 11.5 us)
Async XLA Ops:
  7.2 34.0 %copy-start = (bf16[512,2048]{1,0:T(8,128)(2,1)S(1)}, bf16[512,2048]{1,0:T(8,128)(2,1)}, u32[]{:S(2)}) copy-start(bf16[512,2048]{1,0:T(8,128)(2,1)} %param.8) | copy-start | bytes 6291460
  7.2 165.0 %reduce-scatter.2.cloned.1.call-start = ((), (), s32[]{:S(2)}) async-start(), calls=%async_computation.8 | async-start | bytes 9437184 | tf_op jit(solution)/shard_map/reduce_scatter | solution.py:123
  48.0 0.8 copy-start.3
  99.4 5.4 %copy-start.7 = (s32[32]{0:T(128)S(1)}, s32[32]{0:T(128)}, u32[]{:S(2)}) copy-start(s32[32]{0:T(128)} %param.13) | copy-start | bytes 388
  99.4 5.6 %copy-start.5 = (s32[1024]{0:T(1024)S(1)}, s32[1024]{0:T(1024)}, u32[]{:S(2)}) copy-start(s32[1024]{0:T(1024)} %param.11) | copy-start | bytes 12292
  99.4 49.2 %all-to-all-start.4 = ((bf16[4,128,4096]{2,1,0:T(8,128)(2,1)}), bf16[4,128,4096]{2,1,0:T(8,128)(2,1)}, u32[]{:S(2)}, u32[]{:S(2)}) async-start(bf16[4,128,4096]{2,1,0:T(8,128)(2,1)} %stack.22), calls=%async_computation.5 | async-start | bytes 8388608 | tf_op jit(solution)/shard_map/all_to_all | solution.py:108
  104.8 170.2 %all-gather.12.cloned.1.call-start = ((), (), s32[]{:S(2)}) async-start(), calls=%async_computation.9 | async-start | bytes 4718592 | tf_op jit(solution)/shard_map/all_gather | solution.py:155
  156.1 12.2 %copy-start.6 = (bf16[4096,256]{1,0:T(8,128)(2,1)S(1)}, bf16[4096,256]{1,0:T(8,128)(2,1)}, u32[]{:S(2)}) copy-start(bf16[4096,256]{1,0:T(8,128)(2,1)} %param.10) | copy-start | bytes 6291460
  170.7 52.2 %copy-start.4 = (s32[1024]{0:T(1024)S(1)}, s32[1024]{0:T(1024)}, u32[]{:S(2)}) copy-start(s32[1024]{0:T(1024)} %param.12) | copy-start | bytes 12292
  172.2 53.1 %copy-start.1 = (f32[256,1024]{1,0:T(8,128)S(1)}, f32[256,1024]{1,0:T(8,128)}, u32[]{:S(2)}) copy-start(f32[256,1024]{1,0:T(8,128)} %reduce-scatter.2.cloned.1.call-done) | copy-start | bytes 3145732
  280.9 13.9 %copy-start.2 = (bf16[8,128,512]{2,1,0:T(8,128)(2,1)S(1)}, bf16[8,128,512]{2,1,0:T(8,128)(2,1)}, u32[]{:S(2)}) copy-start(bf16[8,128,512]{2,1,0:T(8,128)(2,1)} %copy.27) | copy-start | bytes 3145732
  280.9 67.8 %all-to-all-start.6 = ((f32[32,32,512]{2,1,0:T(8,128)}), f32[32,32,512]{2,1,0:T(8,128)}, u32[]{:S(2)}, u32[]{:S(2)}) async-start(f32[32,32,512]{2,1,0:T(8,128)} %bitcast.460), calls=%async_computation.7 | async-start | bytes 4194304 | tf_op jit(solution)/shard_map/all_to_all | solution.py:49
Sparse Core Ops, SparseCore 0:
  48.2 99.6 reduce-scatter.1
  226.5 48.3 all-gather.11
